TPU v7x, 32 devices: a whole 2x2x4 slice. The times are simulated.
32 devices in a mesh: expert: 4 (over x, core), shard: 8 (over z, y).
Axes of the slice: x: 2, y: 2, z: 4, core: 2. Of those that a mesh axis runs over, the one named last changes fastest.
Arguments:
- train_down: float32 [16, 6400, 4096], P('expert', None, 'shard'), may hold values from -0.109375 to 0.109375
- other_down: bfloat16 [16, 6400, 4096], P('expert', None, 'shard'), may hold values from -0.0390625 to 0.0390625
- router_weight: float32 [4096, 16], P('shard', 'expert'), may hold values from -0.09375 to 0.09375
- router_gain: float32 [4096], P('shard'), may hold values from 0.25 to 1.75
Outputs:
- ready_down: bfloat16 [16, 6400, 4096], P('expert', 'shard')
- scale_down: float32 [16, 6400], P('expert', 'shard')
- serve_router: bfloat16 [4096, 16], replicated
All inputs are finite; a program needn't handle non-finite values. Where the computation divides by a largest or mean magnitude, that divisor is 1e-20 or more.
Results may differ from a plain program's by a relative error of at most 0.001.
Values may be sent and summed in bfloat16 or wider, within the bound.
A program may use at most 256 MiB of HBM per device.

v0:
```python
import jax
import jax.numpy as jnp
from jax import lax
from jax.sharding import PartitionSpec as P


def per_device(train_down, other_down, router_weight, router_gain):
    latest_down = train_down + other_down.astype(jnp.float32)
    scale_down = lax.pmax(jnp.max(jnp.abs(latest_down), axis=2), "shard")
    narrow_down = (latest_down / jnp.expand_dims(scale_down, 2)).astype(jnp.bfloat16)
    ready_down = lax.all_to_all(narrow_down, "shard", split_axis=1, concat_axis=2, tiled=True)
    scale_down = lax.dynamic_slice_in_dim(
        scale_down, lax.axis_index("shard") * ready_down.shape[1], ready_down.shape[1], axis=1
    )
    part_router = (router_weight * router_gain[:, None]).astype(jnp.bfloat16)
    row_router = lax.all_gather(part_router, "shard", axis=0, tiled=True)
    serve_router = lax.all_gather(row_router, "expert", axis=1, tiled=True)
    return (ready_down, scale_down, serve_router)


def solution(mesh):
    in_specs = (
        P("expert", None, "shard"),
        P("expert", None, "shard"),
        P("shard", "expert"),
        P("shard"),
    )
    out_specs = (P("expert", "shard", None), P("expert", "shard"), P())
    return jax.shard_map(
        per_device, mesh=mesh, in_specs=in_specs, out_specs=out_specs, check_vma=False
    )
```

profile of v0, /device:TPU:0, one launch (start us, length us, event | category | flops | bytes accessed | tf_op | source)
XLA Modules:
  0.0 903.4 jit_solution(8712372053355540380)
XLA Ops:
  7.2 0.0 all-reduce.2.cloned.1.call-start
  7.2 24.2 %abs_reduce_fusion = f32[4,6400]{1,0:T(4,128)S(1)} fusion(f32[4,6400,512]{2,1,0:T(8,128)} %param.4, bf16[4,6400,512]{2,1,0:T(8,128)(2,1)} %param.5), kind=kLoop, calls=%fused_computation.1 | loop fusion | flops 52403200 | bytes 78745600 | tf_op jit(solution)/shard_map/reduce_max | solution.py:9
  31.4 2.3 copy.21
  33.7 0.0 all-reduce.2.cloned.1.call-update
  33.7 135.6 %all-reduce.2.cloned.1.call-done = f32[4,6400]{0,1:T(8,128)} async-done(((f32[4,6400]{0,1:T(8,128)}), f32[4,6400]{0,1:T(8,128)}) %all-reduce.2.cloned.1.call-update) | async-done | bytes 102416 | tf_op jit(solution)/shard_map/pmax | solution.py:9
  169.4 2.4 copy.17
  171.8 34.3 %divide_convert_fusion = bf16[4,6400,512]{2,1,0:T(8,128)(2,1)} fusion(f32[4,6400,512]{2,1,0:T(8,128)} %param.4, bf16[4,6400,512]{2,1,0:T(8,128)(2,1)} %param.5, f32[4,6400]{1,0:T(4,128)S(1)} %copy.17), kind=kLoop, calls=%fused_computation | loop fusion | flops 52428800 | bytes 104960000 | tf_op jit(solution)/shard_map/convert_element_type | solution.py:10
  206.1 33.4 %copy.18 = bf16[4,6400,512]{2,0,1:T(4,128)(2,1)} copy(bf16[4,6400,512]{2,1,0:T(8,128)(2,1)} %divide_convert_fusion) | data formatting | bytes 52428800 | tf_op jit(solution)/shard_map/convert_element_type | solution.py:10
  239.5 0.0 copy-start
  239.5 0.0 copy-start.1
  239.5 6.6 all-to-all-start
  246.1 0.0 copy-done
  246.2 0.0 copy-done.1
  246.2 585.0 %all_gather.6 = bf16[4096,4]{0,1:T(4,128)(2,1)S(1)} all-gather(bf16[512,4]{0,1:T(4,128)(2,1)S(1)} %multiply_convert_fusion), channel_id=1, replica_groups=mesh['expert'=4,'shard'=8] {'shard'}, dimensions={0}, use_global_device_ids=true | all-gather | bytes 36864 | tf_op jit(solution)/shard_map/all_gather | solution.py:16
  831.2 5.4 all-gather
  836.6 0.7 reshape.9
  837.3 1.0 constant_dynamic-slice_fusion
  838.4 0.8 copy.20
  839.1 0.0 all-to-all-done
  839.1 18.2 %copy.19 = bf16[4,800,8,512]{3,2,1,0:T(8,128)(2,1)} copy(bf16[4,800,8,512]{3,0,1,2:T(4,128)(2,1)} %bitcast.1) | data formatting | bytes 52428800 | tf_op jit(solution)/shard_map/all_to_all | solution.py:11
  857.4 39.2 %all_to_all.16 = bf16[4,800,4096]{2,1,0:T(8,128)(2,1)} reshape(bf16[4,800,8,512]{3,2,1,0:T(8,128)(2,1)} %copy.19) | data formatting | bytes 52428800 | tf_op jit(solution)/shard_map/all_to_all | solution.py:11
  (1 shorter events, 0.0 us)
Async XLA Ops:
  7.2 162.2 %all-reduce.2.cloned.1.call-start = ((), (), s32[]{:S(2)}) async-start(), calls=%async_computation.1 | async-start | bytes 6553600 | tf_op jit(solution)/shard_map/pmax | solution.py:9
  239.5 6.7 copy-start
  239.5 6.7 copy-start.1
  239.5 599.6 %all-to-all-start = ((bf16[4,6400,512]{2,0,1:T(4,128)(2,1)}), bf16[4,6400,512]{2,0,1:T(4,128)(2,1)}, u32[]{:S(2)}, u32[]{:S(2)}) async-start(bf16[4,6400,512]{2,0,1:T(4,128)(2,1)} %copy.18), calls=%async_computation | async-start | bytes 52428800 | tf_op jit(solution)/shard_map/all_to_all | solution.py:11
Sparse Core Ops, SparseCore 0:
  33.9 135.4 all-reduce.1
where the time goes:
time: 905 us; the launch traced here: 903 us
  blocking collectives  590 us (65%)
  waiting for transfers between devices  136 us (15%)
  local copies, waits for them, and re-layouts  98 us (11%)
  other arithmetic  58.5 us (6%)
  between operations  14.1 us (2%)
    all_gather x1, blocking collectives, per_device(): row_router = lax.all_gather(part_router, 'shard', axis=0, tiled=True)  585 us
    pmax x1, waiting for transfers between devices, per_device(): scale_down = lax.pmax(jnp.max(jnp.abs(latest_down), axis=2), 'shard')  136 us
    all_to_all x2, local copies, waits for them, and re-layouts, per_device(): lax.all_to_all(narrow_down, 'shard', split_axis=1, concat_axis=2, tiled=T...  57.4 us
    convert_element_type x1, other arithmetic, per_device(): (latest_down / jnp.expand_dims(scale_down, 2)).astype(jnp.bfloat16)  34.3 us
    convert_element_type x1, local copies, waits for them, and re-layouts, per_device(): (latest_down / jnp.expand_dims(scale_down, 2)).astype(jnp.bfloat16)  33.4 us
    reduce_max x1, other arithmetic, per_device(): scale_down = lax.pmax(jnp.max(jnp.abs(latest_down), axis=2), 'shard')  24.2 us
  transfers between devices with their start and end apart: 2, of which 1 were waited for; matrix products, arithmetic and copies ran while one was open for 0% of the time, Pallas kernels for 0%

commit v1 on v0

--- a/solution.py
+++ b/solution.py
@@ -8,7 +8,12 @@
     latest_down = train_down + other_down.astype(jnp.float32)
     scale_down = lax.pmax(jnp.max(jnp.abs(latest_down), axis=2), "shard")
     narrow_down = (latest_down / jnp.expand_dims(scale_down, 2)).astype(jnp.bfloat16)
-    ready_down = lax.all_to_all(narrow_down, "shard", split_axis=1, concat_axis=2, tiled=True)
+    ready_down = jnp.concatenate(
+        lax.all_to_all(
+            jnp.stack(jnp.split(narrow_down, lax.axis_size("shard"), axis=1)), "shard", 0, 0
+        ),
+        axis=2,
+    )
     scale_down = lax.dynamic_slice_in_dim(
         scale_down, lax.axis_index("shard") * ready_down.shape[1], ready_down.shape[1], axis=1
     )

time: 905 us -> 792 us (0.88)
  waiting for transfers between devices: 136 us -> 72.5 us
  local copies, waits for them, and re-layouts: 98 us -> 50.6 us
    pmax x1, waiting for transfers between devices: 136 us -> 72.5 us  [per_device(): scale_down = lax.pmax(jnp.max(jnp.abs(latest_down), axis=2), 'shard')]
    all_to_all x2 -> x0, local copies, waits for them, and re-layouts: 57.4 us -> none  [per_device(): lax.all_to_all(narrow_down, 'shard', split_axis=1, concat_axis=2, tiled=T...]
    convert_element_type x1 -> x0, local copies, waits for them, and re-layouts: 33.4 us -> none  [per_device(): (latest_down / jnp.expand_dims(scale_down, 2)).astype(jnp.bfloat16)]
    unnamed x7 -> x12, local copies, waits for them, and re-layouts: 3.75 us -> 27.5 us
    reshape x0 -> x1, local copies, waits for them, and re-layouts: none -> 17.9 us  [per_device(): jnp.concatenate(lax.all_to_all(jnp.stack(jnp.split(narrow_down, lax.axis_...]
where the time goes in v1:
time: 792 us
  blocking collectives  589 us (74%)
  waiting for transfers between devices  72.5 us (9%)
  other arithmetic  59.2 us (7%)
  local copies, waits for them, and re-layouts  50.6 us (6%)
  between operations  14.1 us (2%)
    all_gather x1, blocking collectives, per_device(): row_router = lax.all_gather(part_router, 'shard', axis=0, tiled=True)  583 us
    pmax x1, waiting for transfers between devices, per_device(): scale_down = lax.pmax(jnp.max(jnp.abs(latest_down), axis=2), 'shard')  72.5 us
    convert_element_type x1, other arithmetic, per_device(): (latest_down / jnp.expand_dims(scale_down, 2)).astype(jnp.bfloat16)  34.4 us
    unnamed x12, local copies, waits for them, and re-layouts  27.5 us
    reduce_max x1, other arithmetic, per_device(): scale_down = lax.pmax(jnp.max(jnp.abs(latest_down), axis=2), 'shard')  24.9 us
    reshape x1, local copies, waits for them, and re-layouts, per_device(): jnp.concatenate(lax.all_to_all(jnp.stack(jnp.split(narrow_down, lax.axis_...  17.9 us
  transfers between devices with their start and end apart: 2, of which 1 were waited for; matrix products, arithmetic and copies ran while one was open for 0% of the time, Pallas kernels for 0%

profile of v1, /device:TPU:0, one launch (start us, length us, event | category | flops | bytes accessed | tf_op | source)
XLA Modules:
  0.0 791.9 jit_solution(10896908688259474292)
XLA Ops:
  7.2 0.0 all-reduce.2.cloned.1.call-start
  7.2 24.9 %abs_reduce_fusion = f32[4,6400]{1,0:T(4,128)} fusion(f32[4,6400,512]{2,1,0:T(8,128)} %param.4, bf16[4,6400,512]{2,1,0:T(8,128)(2,1)} %param.5), kind=kLoop, calls=%fused_computation.1 | loop fusion | flops 52403200 | bytes 78745600 | tf_op jit(solution)/shard_map/reduce_max | solution.py:9
  32.1 0.0 all-reduce.2.cloned.1.call-update
  32.1 72.5 %all-reduce.2.cloned.1.call-done = f32[4,6400]{1,0:T(4,128)} async-done(((f32[4,6400]{1,0:T(4,128)}), f32[4,6400]{1,0:T(4,128)}) %all-reduce.2.cloned.1.call-update) | async-done | bytes 102416 | tf_op jit(solution)/shard_map/pmax | solution.py:9
  104.6 34.4 %divide_convert_fusion = bf16[4,6400,512]{2,1,0:T(8,128)(2,1)} fusion(f32[4,6400,512]{2,1,0:T(8,128)} %param.4, bf16[4,6400,512]{2,1,0:T(8,128)(2,1)} %param.5, f32[4,6400]{1,0:T(4,128)} %all-reduce.2.cloned.1.call-done), kind=kLoop, calls=%fused_computation | loop fusion | flops 52428800 | bytes 104960000 | tf_op jit(solution)/shard_map/convert_element_type | solution.py:10
  139.0 3.8 fusion.7
  142.8 3.8 fusion.6
  146.6 3.8 fusion.5
  150.4 3.8 fusion.4
  154.3 3.9 fusion.3
  158.1 3.8 fusion.2
  162.0 3.8 fusion.1
  165.8 3.8 fusion
  169.6 0.0 copy-start
  169.6 0.0 copy-start.1
  169.6 6.6 all-to-all-start
  176.2 0.0 copy-done
  176.2 0.0 copy-done.1
  176.3 583.4 %all_gather.6 = bf16[4096,4]{0,1:T(4,128)(2,1)S(1)} all-gather(bf16[512,4]{0,1:T(4,128)(2,1)S(1)} %multiply_convert_fusion), channel_id=1, replica_groups=mesh['expert'=4,'shard'=8] {'shard'}, dimensions={0}, use_global_device_ids=true | all-gather | bytes 36864 | tf_op jit(solution)/shard_map/all_gather | solution.py:21
  759.7 5.4 all-gather
  765.1 0.7 reshape.17
  765.8 1.4 constant_dynamic-slice_fusion
  767.2 0.0 all-to-all-done
  767.2 17.9 %copy.9 = bf16[8,4,100,8,512]{4,3,0,2,1:T(8,128)(2,1)} copy(bf16[8,4,100,8,512]{4,3,2,1,0:T(8,128)(2,1)} %bitcast.13) | data formatting | bytes 52428800 | tf_op jit(solution)/shard_map/reshape | solution.py:11
  (1 shorter events, 0.0 us)
Async XLA Ops:
  7.2 97.4 %all-reduce.2.cloned.1.call-start = ((), (), s32[]{:S(2)}) async-start(), calls=%async_computation.1 | async-start | bytes 204800 | tf_op jit(solution)/shard_map/pmax | solution.py:9
  169.6 6.6 copy-start
  169.6 6.6 copy-start.1
  169.6 597.6 %all-to-all-start = ((bf16[8,4,800,512]{3,2,1,0:T(8,128)(2,1)}), bf16[8,4,800,512]{3,2,1,0:T(8,128)(2,1)}, u32[]{:S(2)}, u32[]{:S(2)}) async-start(bf16[8,4,800,512]{3,2,1,0:T(8,128)(2,1)} %fusion), calls=%async_computation | async-start | bytes 52428800 | tf_op jit(solution)/shard_map/all_to_all | solution.py:12
Sparse Core Ops, SparseCore 0:
  32.2 72.3 all-reduce.1
